TPU v7x, 256 devices: a whole 4x4x8 slice. The times are simulated.
256 devices in a mesh: rows: 256 (over y, x, z, core).
Axes of the slice: x: 4, y: 4, z: 8, core: 2. Of those that a mesh axis runs over, the one named last changes fastest.
Arguments:
- start_panel: float32 [8, 262144], P(None, 'rows'), may hold values from -10 to 10, as said below
- diagonal_inverse: bfloat16 [256, 1024, 1024], P('rows'), may hold values from -0.6 to 12.5
- right_factor: bfloat16 [256, 1024, 1024], P('rows'), may hold values from -0.03125 to 0.03125
- left_factor: bfloat16 [256, 1024, 1024], P('rows'), may hold values from -0.03125 to 0.03125
Outputs:
- new_panels: float32 [24, 262144], P(None, 'rows')
- coefficients: float32 [3, 32, 8], replicated
- first_coefficients: float32 [3, 32, 8], replicated
Inputs may be any that keep to these rules, and one draw needn't show every extreme that they name: The rows of start_panel are orthonormal under the inner product divided by 262144, up to float32 rounding.
All inputs are finite; a program needn't handle non-finite values.
Results may differ from a plain program's by a relative error of at most 0.014.
Values sent between devices are 32-bit elements; how exact they have to be, the bound alone decides.
A program may use at most 64 MiB of HBM per device.

v0:
```python
import jax
import jax.numpy as jnp
from jax import lax
from jax.sharding import Mesh
from jax.sharding import PartitionSpec as P

STEPS = 3
BASIS = 32
ROWS = ("rows_0", "rows_1", "rows_2", "rows_3")


epsilon = 1e-06


def passed_along(value, axis, steps):
    count = lax.axis_size(axis)
    initial, last = (max(0, -steps), min(count, count - steps))
    return lax.ppermute(value, axis, [(source, source + steps) for source in range(initial, last)])


def from_everyone(shard, axis):
    size = lax.axis_size(axis)
    return lax.all_to_all(
        jnp.broadcast_to(shard[None], (size, *shard.shape)), axis, 0, 0, tiled=True
    )


def over_copies(shard, axis):
    return from_everyone(shard, axis).sum(axis=0)


def by_axis(shard, axes):
    far, near = axes
    return over_copies(over_copies(shard, near), far)


def packed_total(arrays, axis):
    ends = [0]
    for a in arrays:
        ends.append(ends[-1] + a.size)
    subtotal = by_axis(jnp.concatenate([a.ravel() for a in arrays]), axis)
    return tuple((subtotal[b:e].reshape(a.shape) for a, b, e in zip(arrays, ends, ends[1:])))


def cyclic_solve(current, diagonal_inverse, right_factor, left_factor):
    levels = lax.axis_size(ROWS).bit_length() - 1
    updated = current
    for height in range(levels):
        distance = 2**height
        lowered = updated.astype(jnp.bfloat16)
        upward = jnp.dot(lowered, right_factor[0], preferred_element_type=jnp.float32)
        downward = jnp.dot(lowered, left_factor[0], preferred_element_type=jnp.float32)
        from_below = passed_along(upward, ROWS, distance)
        from_above = passed_along(downward, ROWS, -distance)
        updated = updated - from_below - from_above
    return jnp.dot(
        updated.astype(jnp.bfloat16), diagonal_inverse[0], preferred_element_type=jnp.float32
    )


def product(left, right):
    return jnp.dot(left, right, precision=lax.Precision.HIGHEST)


def inner_rows(left, right):
    return jnp.dot(left, right.T, precision=lax.Precision.HIGHEST)


def extend_gram(previous, cross_gram, width):
    if previous is None:
        return cross_gram
    upper = jnp.concatenate([previous, cross_gram[:-width]], 1)
    return jnp.concatenate([upper, cross_gram.T], 0)


def body(start_panel, diagonal_inverse, right_factor, left_factor):
    width = start_panel.shape[0]
    unknowns = start_panel.shape[1] * lax.axis_size(ROWS)
    krylov_basis = start_panel
    current = start_panel
    gram_basis = None
    produced = []
    coefficients = []
    firsts = []
    for iteration in range(STEPS):
        images = cyclic_solve(current, diagonal_inverse, right_factor, left_factor)
        height = krylov_basis.shape[0]
        reduced = packed_total(
            (
                inner_rows(krylov_basis, images),
                inner_rows(krylov_basis, current),
                inner_rows(images, images),
            ),
            ("rows_0", ("rows_1", "rows_2", "rows_3")),
        )
        coef_first = reduced[0] / unknowns
        gram_basis = extend_gram(gram_basis, reduced[1] / unknowns, width)
        coef_second = coef_first - product(gram_basis, coef_first)
        combined = coef_first + coef_second
        remainder = images - product(combined.T, krylov_basis)
        gram_new = (
            reduced[2] / unknowns
            - product(combined.T, coef_first)
            - product(coef_first.T, combined)
        )
        gram_new = gram_new + product(combined.T, product(gram_basis, combined))
        gram_new = gram_new + epsilon * jnp.eye(width, dtype=jnp.float32)
        lower_factor = jnp.linalg.cholesky(gram_new)
        fresh = jax.scipy.linalg.solve_triangular(lower_factor, remainder, lower=True)
        column_block = jnp.zeros((BASIS, width), jnp.float32)
        column_block = column_block.at[:height].set(combined)
        column_block = column_block.at[height : height + width].set(lower_factor.T)
        first_block = jnp.zeros((BASIS, width), jnp.float32).at[:height].set(coef_first)
        produced.append(fresh)
        coefficients.append(column_block)
        firsts.append(first_block)
        krylov_basis = jnp.concatenate([krylov_basis, fresh], 0)
        current = fresh
    return (jnp.concatenate(produced, 0), jnp.stack(coefficients), jnp.stack(firsts))


def solution(mesh):
    finer = Mesh(mesh.devices.reshape(4, 4, 8, 2), ("rows_0", "rows_1", "rows_2", "rows_3"))
    placed = (P(None, ROWS), P(ROWS, None, None), P(ROWS, None, None), P(ROWS, None, None))
    return jax.shard_map(
        body, mesh=finer, in_specs=placed, out_specs=(P(None, ROWS), P(), P()), check_vma=False
    )
```

profile of v0, /device:TPU:1, one launch (start us, length us, event | category | flops | bytes accessed | tf_op | source)
XLA Modules:
  0.0 404.4 jit_solution(5729166243783789327)
XLA Ops:
  3.4 4.9 %collective-permute-start = (f32[8,1024]{1,0:T(8,128)S(1)}, f32[8,1024]{1,0:T(8,128)S(1)}, u32[]{:S(2)}, u32[]{:S(2)}) collective-permute-start(f32[8,1024]{1,0:T(8,128)S(1)} %fusion.100), channel_id=1, source_target_pairs={{0,1},{1,2},{2,3},{3,4},{4,5},{5,6},{6,7},{7,8},{8,9},{9,10},{10,1... | collective-permute-start | bytes 98312 | tf_op jit(solution)/shard_map/ppermute | solution.py:18
  23.9 7.1 %collective-permute-start.4 = (f32[8,1024]{1,0:T(8,128)S(1)}, f32[8,1024]{1,0:T(8,128)S(1)}, u32[]{:S(2)}, u32[]{:S(2)}) collective-permute-start(f32[8,1024]{1,0:T(8,128)S(1)} %fusion.96), channel_id=1, source_target_pairs={{0,4},{1,5},{2,6},{3,7},{4,8},{5,9},{6,10},{7,11},{8,12},{9,13},{1... | collective-permute-start | bytes 98312 | tf_op jit(solution)/shard_map/ppermute | solution.py:18
  32.3 4.2 %collective-permute-done.5 = f32[8,1024]{1,0:T(8,128)S(1)} collective-permute-done((f32[8,1024]{1,0:T(8,128)S(1)}, f32[8,1024]{1,0:T(8,128)S(1)}, u32[]{:S(2)}, u32[]{:S(2)}) %collective-permute-start.5) | collective-permute-done | bytes 32800 | tf_op jit(solution)/shard_map/ppermute | solution.py:18
  42.3 7.3 %collective-permute-done.7 = f32[8,1024]{1,0:T(8,128)S(1)} collective-permute-done((f32[8,1024]{1,0:T(8,128)S(1)}, f32[8,1024]{1,0:T(8,128)S(1)}, u32[]{:S(2)}, u32[]{:S(2)}) %collective-permute-start.7) | collective-permute-done | bytes 32800 | tf_op jit(solution)/shard_map/ppermute | solution.py:18
  58.9 10.0 %collective-permute-start.10 = (f32[8,1024]{1,0:T(8,128)S(1)}, f32[8,1024]{1,0:T(8,128)S(1)}, u32[]{:S(2)}, u32[]{:S(2)}) collective-permute-start(f32[8,1024]{1,0:T(8,128)S(1)} %fusion.90), channel_id=1, source_target_pairs={{0,32},{1,33},{2,34},{3,35},{4,36},{5,37},{6,38},{7,39},{8,40},{9,... | collective-permute-start | bytes 98312 | tf_op jit(solution)/shard_map/ppermute | solution.py:18
  70.2 4.9 %collective-permute-done.11 = f32[8,1024]{1,0:T(8,128)S(1)} collective-permute-done((f32[8,1024]{1,0:T(8,128)S(1)}, f32[8,1024]{1,0:T(8,128)S(1)}, u32[]{:S(2)}, u32[]{:S(2)}) %collective-permute-start.11) | collective-permute-done | bytes 32800 | tf_op jit(solution)/shard_map/ppermute | solution.py:18
  89.9 4.6 %collective-permute-done.15 = f32[8,1024]{1,0:T(8,128)S(1)} collective-permute-done((f32[8,1024]{1,0:T(8,128)S(1)}, f32[8,1024]{1,0:T(8,128)S(1)}, u32[]{:S(2)}, u32[]{:S(2)}) %collective-permute-start.15) | collective-permute-done | bytes 32800 | tf_op jit(solution)/shard_map/ppermute | solution.py:18
  97.2 28.4 %all_to_all.36 = f32[64,1,192]{2,1,0:T(1,128)S(1)} all-to-all(f32[64,1,192]{2,1,0:T(1,128)S(1)} %broadcast_in_dim.13), channel_id=1, replica_groups=mesh['rows_0'=4,'rows_1'=4,'rows_2'=8,'rows_3'=2] {'rows_1','rows_2','ro..., dimensions={0} | all-to-all | bytes 98304 | tf_op jit(solution)/shard_map/all_to_all | solution.py:23
  125.7 6.5 %all_to_all.37 = f32[4,1,192]{2,1,0:T(1,128)S(1)} all-to-all(f32[4,1,192]{2,1,0:T(1,128)S(1)} %broadcast_in_dim.14), channel_id=1, replica_groups=mesh['rows_0'=4,'rows_1'=4,'rows_2'=8,'rows_3'=2] {'rows_0'}, dimensions={0} | all-to-all | bytes 6144 | tf_op jit(solution)/shard_map/all_to_all | solution.py:23
  166.0 7.5 %collective-permute-start.22 = (f32[8,1024]{1,0:T(8,128)S(1)}, f32[8,1024]{1,0:T(8,128)S(1)}, u32[]{:S(2)}, u32[]{:S(2)}) collective-permute-start(f32[8,1024]{1,0:T(8,128)S(1)} %fusion.78), channel_id=1, source_target_pairs={{0,8},{1,9},{2,10},{3,11},{4,12},{5,13},{6,14},{7,15},{8,16},{9,17... | collective-permute-start | bytes 98312 | tf_op jit(solution)/shard_map/ppermute | solution.py:18
  174.8 7.3 %collective-permute-done.23 = f32[8,1024]{1,0:T(8,128)S(1)} collective-permute-done((f32[8,1024]{1,0:T(8,128)S(1)}, f32[8,1024]{1,0:T(8,128)S(1)}, u32[]{:S(2)}, u32[]{:S(2)}) %collective-permute-start.23) | collective-permute-done | bytes 32800 | tf_op jit(solution)/shard_map/ppermute | solution.py:18
  190.7 10.5 %collective-permute-start.26 = (f32[8,1024]{1,0:T(8,128)S(1)}, f32[8,1024]{1,0:T(8,128)S(1)}, u32[]{:S(2)}, u32[]{:S(2)}) collective-permute-start(f32[8,1024]{1,0:T(8,128)S(1)} %fusion.74), channel_id=1, source_target_pairs={{0,32},{1,33},{2,34},{3,35},{4,36},{5,37},{6,38},{7,39},{8,40},{9,... | collective-permute-start | bytes 98312 | tf_op jit(solution)/shard_map/ppermute | solution.py:18
  202.5 4.9 %collective-permute-done.27 = f32[8,1024]{1,0:T(8,128)S(1)} collective-permute-done((f32[8,1024]{1,0:T(8,128)S(1)}, f32[8,1024]{1,0:T(8,128)S(1)}, u32[]{:S(2)}, u32[]{:S(2)}) %collective-permute-start.27) | collective-permute-done | bytes 32800 | tf_op jit(solution)/shard_map/ppermute | solution.py:18
  221.1 4.6 %collective-permute-done.31 = f32[8,1024]{1,0:T(8,128)S(1)} collective-permute-done((f32[8,1024]{1,0:T(8,128)S(1)}, f32[8,1024]{1,0:T(8,128)S(1)}, u32[]{:S(2)}, u32[]{:S(2)}) %collective-permute-start.31) | collective-permute-done | bytes 32800 | tf_op jit(solution)/shard_map/ppermute | solution.py:18
  228.2 28.8 %all_to_all.38 = f32[64,1,320]{2,1,0:T(1,128)S(1)} all-to-all(f32[64,1,320]{2,1,0:T(1,128)S(1)} %broadcast_in_dim.15), channel_id=1, replica_groups=mesh['rows_0'=4,'rows_1'=4,'rows_2'=8,'rows_3'=2] {'rows_1','rows_2','ro..., dimensions={0} | all-to-all | bytes 163840 | tf_op jit(solution)/shard_map/all_to_all | solution.py:23
  257.2 6.5 %all_to_all.39 = f32[4,1,320]{2,1,0:T(1,128)S(1)} all-to-all(f32[4,1,320]{2,1,0:T(1,128)S(1)} %broadcast_in_dim.16), channel_id=1, replica_groups=mesh['rows_0'=4,'rows_1'=4,'rows_2'=8,'rows_3'=2] {'rows_0'}, dimensions={0} | all-to-all | bytes 10240 | tf_op jit(solution)/shard_map/all_to_all | solution.py:23
  292.8 4.2 %collective-permute-done.37 = f32[8,1024]{1,0:T(8,128)S(1)} collective-permute-done((f32[8,1024]{1,0:T(8,128)S(1)}, f32[8,1024]{1,0:T(8,128)S(1)}, u32[]{:S(2)}, u32[]{:S(2)}) %collective-permute-start.37) | collective-permute-done | bytes 32800 | tf_op jit(solution)/shard_map/ppermute | solution.py:18
  297.8 7.4 %collective-permute-start.38 = (f32[8,1024]{1,0:T(8,128)S(1)}, f32[8,1024]{1,0:T(8,128)S(1)}, u32[]{:S(2)}, u32[]{:S(2)}) collective-permute-start(f32[8,1024]{1,0:T(8,128)S(1)} %fusion.62), channel_id=1, source_target_pairs={{0,8},{1,9},{2,10},{3,11},{4,12},{5,13},{6,14},{7,15},{8,16},{9,17... | collective-permute-start | bytes 98312 | tf_op jit(solution)/shard_map/ppermute | solution.py:18
  306.5 7.3 %collective-permute-done.39 = f32[8,1024]{1,0:T(8,128)S(1)} collective-permute-done((f32[8,1024]{1,0:T(8,128)S(1)}, f32[8,1024]{1,0:T(8,128)S(1)}, u32[]{:S(2)}, u32[]{:S(2)}) %collective-permute-start.39) | collective-permute-done | bytes 32800 | tf_op jit(solution)/shard_map/ppermute | solution.py:18
  322.4 10.4 %collective-permute-start.42 = (f32[8,1024]{1,0:T(8,128)S(1)}, f32[8,1024]{1,0:T(8,128)S(1)}, u32[]{:S(2)}, u32[]{:S(2)}) collective-permute-start(f32[8,1024]{1,0:T(8,128)S(1)} %fusion.58), channel_id=1, source_target_pairs={{0,32},{1,33},{2,34},{3,35},{4,36},{5,37},{6,38},{7,39},{8,40},{9,... | collective-permute-start | bytes 98312 | tf_op jit(solution)/shard_map/ppermute | solution.py:18
  334.1 4.9 %collective-permute-done.43 = f32[8,1024]{1,0:T(8,128)S(1)} collective-permute-done((f32[8,1024]{1,0:T(8,128)S(1)}, f32[8,1024]{1,0:T(8,128)S(1)}, u32[]{:S(2)}, u32[]{:S(2)}) %collective-permute-start.43) | collective-permute-done | bytes 32800 | tf_op jit(solution)/shard_map/ppermute | solution.py:18
  352.8 4.5 %collective-permute-done.47 = f32[8,1024]{1,0:T(8,128)S(1)} collective-permute-done((f32[8,1024]{1,0:T(8,128)S(1)}, f32[8,1024]{1,0:T(8,128)S(1)}, u32[]{:S(2)}, u32[]{:S(2)}) %collective-permute-start.47) | collective-permute-done | bytes 32800 | tf_op jit(solution)/shard_map/ppermute | solution.py:18
  360.7 18.9 %all-to-all-start.4 = ((f32[64,1,448]{2,1,0:T(1,128)}), f32[64,1,448]{2,1,0:T(1,128)S(1)}, u32[]{:S(2)}, u32[]{:S(2)}) async-start(f32[64,1,448]{2,1,0:T(1,128)} %broadcast_in_dim.17), calls=%async_computation.4 | async-start | bytes 262144 | tf_op jit(solution)/shard_map/all_to_all | solution.py:23
  379.9 10.0 %all-to-all-done.4 = f32[64,1,448]{2,1,0:T(1,128)S(1)} async-done(((f32[64,1,448]{2,1,0:T(1,128)}), f32[64,1,448]{2,1,0:T(1,128)S(1)}, u32[]{:S(2)}, u32[]{:S(2)}) %all-to-all-start.4) | async-done | bytes 114720 | tf_op jit(solution)/shard_map/all_to_all | solution.py:23
  (277 shorter events, 187.6 us)
Async XLA Ops:
  3.4 7.3 %collective-permute-start = (f32[8,1024]{1,0:T(8,128)S(1)}, f32[8,1024]{1,0:T(8,128)S(1)}, u32[]{:S(2)}, u32[]{:S(2)}) collective-permute-start(f32[8,1024]{1,0:T(8,128)S(1)} %fusion.100), channel_id=1, source_target_pairs={{0,1},{1,2},{2,3},{3,4},{4,5},{5,6},{6,7},{7,8},{8,9},{9,10},{10,1... | collective-permute-start | bytes 98312 | tf_op jit(solution)/shard_map/ppermute | solution.py:18
  23.9 8.4 %collective-permute-start.4 = (f32[8,1024]{1,0:T(8,128)S(1)}, f32[8,1024]{1,0:T(8,128)S(1)}, u32[]{:S(2)}, u32[]{:S(2)}) collective-permute-start(f32[8,1024]{1,0:T(8,128)S(1)} %fusion.96), channel_id=1, source_target_pairs={{0,4},{1,5},{2,6},{3,7},{4,8},{5,9},{6,10},{7,11},{8,12},{9,13},{1... | collective-permute-start | bytes 98312 | tf_op jit(solution)/shard_map/ppermute | solution.py:18
  31.0 5.6 %collective-permute-start.5 = (f32[8,1024]{1,0:T(8,128)S(1)}, f32[8,1024]{1,0:T(8,128)S(1)}, u32[]{:S(2)}, u32[]{:S(2)}) collective-permute-start(f32[8,1024]{1,0:T(8,128)S(1)} %fusion.48), channel_id=1, source_target_pairs={{4,0},{5,1},{6,2},{7,3},{8,4},{9,5},{10,6},{11,7},{12,8},{13,9},{1... | collective-permute-start | bytes 98312 | tf_op jit(solution)/shard_map/ppermute | solution.py:18
  41.0 8.6 %collective-permute-start.7 = (f32[8,1024]{1,0:T(8,128)S(1)}, f32[8,1024]{1,0:T(8,128)S(1)}, u32[]{:S(2)}, u32[]{:S(2)}) collective-permute-start(f32[8,1024]{1,0:T(8,128)S(1)} %fusion.46), channel_id=1, source_target_pairs={{8,0},{9,1},{10,2},{11,3},{12,4},{13,5},{14,6},{15,7},{16,8},{17,9... | collective-permute-start | bytes 98312 | tf_op jit(solution)/shard_map/ppermute | solution.py:18
  58.9 11.3 %collective-permute-start.10 = (f32[8,1024]{1,0:T(8,128)S(1)}, f32[8,1024]{1,0:T(8,128)S(1)}, u32[]{:S(2)}, u32[]{:S(2)}) collective-permute-start(f32[8,1024]{1,0:T(8,128)S(1)} %fusion.90), channel_id=1, source_target_pairs={{0,32},{1,33},{2,34},{3,35},{4,36},{5,37},{6,38},{7,39},{8,40},{9,... | collective-permute-start | bytes 98312 | tf_op jit(solution)/shard_map/ppermute | solution.py:18
  68.9 6.2 %collective-permute-start.11 = (f32[8,1024]{1,0:T(8,128)S(1)}, f32[8,1024]{1,0:T(8,128)S(1)}, u32[]{:S(2)}, u32[]{:S(2)}) collective-permute-start(f32[8,1024]{1,0:T(8,128)S(1)} %fusion.42), channel_id=1, source_target_pairs={{32,0},{33,1},{34,2},{35,3},{36,4},{37,5},{38,6},{39,7},{40,8},{41... | collective-permute-start | bytes 98312 | tf_op jit(solution)/shard_map/ppermute | solution.py:18
  84.4 5.4 %collective-permute-start.14 = (f32[8,1024]{1,0:T(8,128)S(1)}, f32[8,1024]{1,0:T(8,128)S(1)}, u32[]{:S(2)}, u32[]{:S(2)}) collective-permute-start(f32[8,1024]{1,0:T(8,128)S(1)} %fusion.86), channel_id=1, source_target_pairs={{0,128},{1,129},{2,130},{3,131},{4,132},{5,133},{6,134},{7,135},{8... | collective-permute-start | bytes 98312 | tf_op jit(solution)/shard_map/ppermute | solution.py:18
  88.3 6.2 %collective-permute-start.15 = (f32[8,1024]{1,0:T(8,128)S(1)}, f32[8,1024]{1,0:T(8,128)S(1)}, u32[]{:S(2)}, u32[]{:S(2)}) collective-permute-start(f32[8,1024]{1,0:T(8,128)S(1)} %fusion.38), channel_id=1, source_target_pairs={{128,0},{129,1},{130,2},{131,3},{132,4},{133,5},{134,6},{135,7},{1... | collective-permute-start | bytes 98312 | tf_op jit(solution)/shard_map/ppermute | solution.py:18
  138.4 5.8 %collective-permute-start.16 = (f32[8,1024]{1,0:T(8,128)S(1)}, f32[8,1024]{1,0:T(8,128)S(1)}, u32[]{:S(2)}, u32[]{:S(2)}) collective-permute-start(f32[8,1024]{1,0:T(8,128)S(1)} %fusion.84), channel_id=1, source_target_pairs={{0,1},{1,2},{2,3},{3,4},{4,5},{5,6},{6,7},{7,8},{8,9},{9,10},{10,1... | collective-permute-start | bytes 98312 | tf_op jit(solution)/shard_map/ppermute | solution.py:18
  159.6 5.6 %collective-permute-start.21 = (f32[8,1024]{1,0:T(8,128)S(1)}, f32[8,1024]{1,0:T(8,128)S(1)}, u32[]{:S(2)}, u32[]{:S(2)}) collective-permute-start(f32[8,1024]{1,0:T(8,128)S(1)} %fusion.32), channel_id=1, source_target_pairs={{4,0},{5,1},{6,2},{7,3},{8,4},{9,5},{10,6},{11,7},{12,8},{13,9},{1... | collective-permute-start | bytes 98312 | tf_op jit(solution)/shard_map/ppermute | solution.py:18
  166.0 8.8 %collective-permute-start.22 = (f32[8,1024]{1,0:T(8,128)S(1)}, f32[8,1024]{1,0:T(8,128)S(1)}, u32[]{:S(2)}, u32[]{:S(2)}) collective-permute-start(f32[8,1024]{1,0:T(8,128)S(1)} %fusion.78), channel_id=1, source_target_pairs={{0,8},{1,9},{2,10},{3,11},{4,12},{5,13},{6,14},{7,15},{8,16},{9,17... | collective-permute-start | bytes 98312 | tf_op jit(solution)/shard_map/ppermute | solution.py:18
  173.5 8.6 %collective-permute-start.23 = (f32[8,1024]{1,0:T(8,128)S(1)}, f32[8,1024]{1,0:T(8,128)S(1)}, u32[]{:S(2)}, u32[]{:S(2)}) collective-permute-start(f32[8,1024]{1,0:T(8,128)S(1)} %fusion.30), channel_id=1, source_target_pairs={{8,0},{9,1},{10,2},{11,3},{12,4},{13,5},{14,6},{15,7},{16,8},{17,9... | collective-permute-start | bytes 98312 | tf_op jit(solution)/shard_map/ppermute | solution.py:18
  190.7 11.8 %collective-permute-start.26 = (f32[8,1024]{1,0:T(8,128)S(1)}, f32[8,1024]{1,0:T(8,128)S(1)}, u32[]{:S(2)}, u32[]{:S(2)}) collective-permute-start(f32[8,1024]{1,0:T(8,128)S(1)} %fusion.74), channel_id=1, source_target_pairs={{0,32},{1,33},{2,34},{3,35},{4,36},{5,37},{6,38},{7,39},{8,40},{9,... | collective-permute-start | bytes 98312 | tf_op jit(solution)/shard_map/ppermute | solution.py:18
  201.2 6.2 %collective-permute-start.27 = (f32[8,1024]{1,0:T(8,128)S(1)}, f32[8,1024]{1,0:T(8,128)S(1)}, u32[]{:S(2)}, u32[]{:S(2)}) collective-permute-start(f32[8,1024]{1,0:T(8,128)S(1)} %fusion.26), channel_id=1, source_target_pairs={{32,0},{33,1},{34,2},{35,3},{36,4},{37,5},{38,6},{39,7},{40,8},{41... | collective-permute-start | bytes 98312 | tf_op jit(solution)/shard_map/ppermute | solution.py:18
  219.5 6.2 %collective-permute-start.31 = (f32[8,1024]{1,0:T(8,128)S(1)}, f32[8,1024]{1,0:T(8,128)S(1)}, u32[]{:S(2)}, u32[]{:S(2)}) collective-permute-start(f32[8,1024]{1,0:T(8,128)S(1)} %fusion.22), channel_id=1, source_target_pairs={{128,0},{129,1},{130,2},{131,3},{132,4},{133,5},{134,6},{135,7},{1... | collective-permute-start | bytes 98312 | tf_op jit(solution)/shard_map/ppermute | solution.py:18
  270.1 5.9 %collective-permute-start.32 = (f32[8,1024]{1,0:T(8,128)S(1)}, f32[8,1024]{1,0:T(8,128)S(1)}, u32[]{:S(2)}, u32[]{:S(2)}) collective-permute-start(f32[8,1024]{1,0:T(8,128)S(1)} %fusion.68), channel_id=1, source_target_pairs={{0,1},{1,2},{2,3},{3,4},{4,5},{5,6},{6,7},{7,8},{8,9},{9,10},{10,1... | collective-permute-start | bytes 98312 | tf_op jit(solution)/shard_map/ppermute | solution.py:18
  291.5 5.6 %collective-permute-start.37 = (f32[8,1024]{1,0:T(8,128)S(1)}, f32[8,1024]{1,0:T(8,128)S(1)}, u32[]{:S(2)}, u32[]{:S(2)}) collective-permute-start(f32[8,1024]{1,0:T(8,128)S(1)} %fusion.16), channel_id=1, source_target_pairs={{4,0},{5,1},{6,2},{7,3},{8,4},{9,5},{10,6},{11,7},{12,8},{13,9},{1... | collective-permute-start | bytes 98312 | tf_op jit(solution)/shard_map/ppermute | solution.py:18
  297.8 8.7 %collective-permute-start.38 = (f32[8,1024]{1,0:T(8,128)S(1)}, f32[8,1024]{1,0:T(8,128)S(1)}, u32[]{:S(2)}, u32[]{:S(2)}) collective-permute-start(f32[8,1024]{1,0:T(8,128)S(1)} %fusion.62), channel_id=1, source_target_pairs={{0,8},{1,9},{2,10},{3,11},{4,12},{5,13},{6,14},{7,15},{8,16},{9,17... | collective-permute-start | bytes 98312 | tf_op jit(solution)/shard_map/ppermute | solution.py:18
  305.2 8.6 %collective-permute-start.39 = (f32[8,1024]{1,0:T(8,128)S(1)}, f32[8,1024]{1,0:T(8,128)S(1)}, u32[]{:S(2)}, u32[]{:S(2)}) collective-permute-start(f32[8,1024]{1,0:T(8,128)S(1)} %fusion.14), channel_id=1, source_target_pairs={{8,0},{9,1},{10,2},{11,3},{12,4},{13,5},{14,6},{15,7},{16,8},{17,9... | collective-permute-start | bytes 98312 | tf_op jit(solution)/shard_map/ppermute | solution.py:18
  322.4 11.7 %collective-permute-start.42 = (f32[8,1024]{1,0:T(8,128)S(1)}, f32[8,1024]{1,0:T(8,128)S(1)}, u32[]{:S(2)}, u32[]{:S(2)}) collective-permute-start(f32[8,1024]{1,0:T(8,128)S(1)} %fusion.58), channel_id=1, source_target_pairs={{0,32},{1,33},{2,34},{3,35},{4,36},{5,37},{6,38},{7,39},{8,40},{9,... | collective-permute-start | bytes 98312 | tf_op jit(solution)/shard_map/ppermute | solution.py:18
  332.8 6.2 %collective-permute-start.43 = (f32[8,1024]{1,0:T(8,128)S(1)}, f32[8,1024]{1,0:T(8,128)S(1)}, u32[]{:S(2)}, u32[]{:S(2)}) collective-permute-start(f32[8,1024]{1,0:T(8,128)S(1)} %fusion.10), channel_id=1, source_target_pairs={{32,0},{33,1},{34,2},{35,3},{36,4},{37,5},{38,6},{39,7},{40,8},{41... | collective-permute-start | bytes 98312 | tf_op jit(solution)/shard_map/ppermute | solution.py:18
  351.2 6.2 %collective-permute-start.47 = (f32[8,1024]{1,0:T(8,128)S(1)}, f32[8,1024]{1,0:T(8,128)S(1)}, u32[]{:S(2)}, u32[]{:S(2)}) collective-permute-start(f32[8,1024]{1,0:T(8,128)S(1)} %fusion.6), channel_id=1, source_target_pairs={{128,0},{129,1},{130,2},{131,3},{132,4},{133,5},{134,6},{135,7},{1... | collective-permute-start | bytes 98312 | tf_op jit(solution)/shard_map/ppermute | solution.py:18
  360.7 29.2 %all-to-all-start.4 = ((f32[64,1,448]{2,1,0:T(1,128)}), f32[64,1,448]{2,1,0:T(1,128)S(1)}, u32[]{:S(2)}, u32[]{:S(2)}) async-start(f32[64,1,448]{2,1,0:T(1,128)} %broadcast_in_dim.17), calls=%async_computation.4 | async-start | bytes 262144 | tf_op jit(solution)/shard_map/all_to_all | solution.py:23
  390.6 7.4 %all-to-all-start.5 = ((f32[4,1,448]{2,1,0:T(1,128)}), f32[4,1,448]{2,1,0:T(1,128)S(1)}, u32[]{:S(2)}, u32[]{:S(2)}) async-start(f32[4,1,448]{2,1,0:T(1,128)} %broadcast_in_dim.18), calls=%async_computation.5 | async-start | bytes 16384 | tf_op jit(solution)/shard_map/all_to_all | solution.py:23
  (31 other events, 139.0 us)
where the time goes:
time: 406 us; the launch traced here: 404 us
  starting transfers between devices  167 us (41%)
  waiting for transfers between devices  117 us (29%)
  blocking collectives  70.2 us (17%)
  matrix products  30.6 us (8%)
  other arithmetic  10.2 us (3%)
  local copies, waits for them, and re-layouts  8.73 us (2%)
    ppermute x48, starting transfers between devices, passed_along(): lax.ppermute(value, axis, [(source, source + steps) for source in range(i...  144 us
    ppermute x48, waiting for transfers between devices, passed_along(): lax.ppermute(value, axis, [(source, source + steps) for source in range(i...  103 us
    all_to_all x4, blocking collectives, from_everyone(): lax.all_to_all(jnp.broadcast_to(shard[None], (size, *shard.shape)), axis,...  70.2 us
    all_to_all x2, starting transfers between devices, from_everyone(): lax.all_to_all(jnp.broadcast_to(shard[None], (size, *shard.shape)), axis,...  22.1 us
    all_to_all x2, waiting for transfers between devices, from_everyone(): lax.all_to_all(jnp.broadcast_to(shard[None], (size, *shard.shape)), axis,...  13.7 us
    dot_general x24, matrix products, cyclic_solve(): jnp.dot(lowered, right_factor[0], preferred_element_type=jnp.float32)  9.95 us
    dot_general x24, matrix products, cyclic_solve(): jnp.dot(lowered, left_factor[0], preferred_element_type=jnp.float32)  9.23 us
  transfers between devices with their start and end apart: 50, of which 26 were waited for; matrix products, arithmetic and copies ran while one was open for 0% of the time, Pallas kernels for 0%

commit v1 on v0

v1 whole, which is shorter than its diff:
```python
import functools

import jax
import jax.numpy as jnp
from jax import lax
from jax.experimental import pallas as pl
from jax.experimental.pallas import tpu as pltpu
from jax.sharding import PartitionSpec as P

STEPS = 3
BASIS = 32
PANEL = 8
CHUNKS = 4
EPSILON = 1e-06
MESH = pl.DeviceIdType.MESH


def split(values):
    leading = values.astype(jnp.bfloat16).astype(jnp.float32)
    return jnp.concatenate([leading, values - leading], 0).astype(jnp.bfloat16)


def times(pair, matrix):
    both = jnp.dot(pair, matrix, preferred_element_type=jnp.float32)
    return both[:PANEL] + both[PANEL:]


def combine(weights, rows_ref):
    total = weights[:, 0:1] * rows_ref[0:1, :]
    for b in range(1, BASIS):
        total = total + weights[:, b : b + 1] * rows_ref[b : b + 1, :]
    return total


def kernel(
    n,
    group,
    hooks,
    start_hbm,
    diagonal_hbm,
    right_hbm,
    left_hbm,
    panels_ref,
    coefficients_ref,
    firsts_ref,
    factors,
    diagonal,
    state,
    outgoing,
    incoming,
    basis,
    images,
    mixing,
    gram,
    near_parts,
    far_parts,
    load_sems,
    send_sems,
    receive_sems,
    near_send,
    near_receive,
    far_send,
    far_receive,
):
    me = lax.axis_index("rows")
    columns = state.shape[1]
    width = columns // CHUNKS
    levels = n.bit_length() - 1
    unknowns = n * columns
    others = n // group
    spot = lax.rem(me, group)
    lane_start = me - spot
    plane = me // group

    def peer(offset):
        return lax.rem(me + (offset + n), n)

    loads = [
        pltpu.make_async_copy(right_hbm.at[0], factors.at[0], load_sems.at[0]),
        pltpu.make_async_copy(left_hbm.at[0], factors.at[1], load_sems.at[1]),
        pltpu.make_async_copy(start_hbm, state, load_sems.at[2]),
        pltpu.make_async_copy(diagonal_hbm.at[0], diagonal, load_sems.at[3]),
    ]
    for load in (loads[2], loads[0], loads[1], loads[3]):
        load.start()

    barrier = pltpu.get_barrier_semaphore()
    near = [lane_start + lax.rem(spot + k, group) for k in range(1, group)]
    far = [spot + group * lax.rem(plane + k, others) for k in range(1, others)]
    across = []
    distance = 1
    while distance < group:
        across += [peer(distance), peer(-distance)]
        distance *= 2
    for target in near + far + across:
        pl.semaphore_signal(barrier, inc=1, device_id=(target,), device_id_type=MESH)

    row8 = lax.broadcasted_iota(jnp.int32, (PANEL, BASIS), 0)
    lane8 = lax.broadcasted_iota(jnp.int32, (PANEL, BASIS), 1)
    basis[...] = jnp.zeros_like(basis)
    images[...] = jnp.zeros_like(images)
    mixing[...] = jnp.where(lane8 == row8, 1.0, 0.0)
    loads[2].wait()
    basis[PANEL : 2 * PANEL, :] = state[...]
    pl.semaphore_wait(barrier, len(near) + len(far) + len(across))
    loads[0].wait()
    loads[1].wait()

    def send(solve, level, chunk):
        slot = solve * levels + level
        parity = level % 2
        distance = 2**level
        last = level == levels - 1
        for way, offset in ((0, distance),) if last else ((0, distance), (1, -distance)):
            pltpu.make_async_remote_copy(
                src_ref=outgoing.at[parity, chunk, way],
                dst_ref=incoming.at[slot, chunk, way],
                send_sem=send_sems.at[parity],
                recv_sem=receive_sems.at[slot, chunk],
                device_id=(peer(offset),),
                device_id_type=MESH,
            ).start()

    def sent(level):
        parity = level % 2
        whole = outgoing.at[parity, :, 0] if level == levels - 1 else outgoing.at[parity]
        pltpu.make_async_copy(whole, whole, send_sems.at[parity]).wait()

    def received(solve, level, chunk):
        slot = solve * levels + level
        distance = 2**level
        place = slice(chunk * width, (chunk + 1) * width)
        if level == levels - 1:
            arrived = incoming.at[slot, chunk, 0]
        else:
            arrived = incoming.at[slot, chunk]
        pltpu.make_async_copy(arrived, arrived, receive_sems.at[slot, chunk]).wait()
        value = state[:, place]
        if level == levels - 1:
            value = value - incoming[slot, chunk, 0]
        else:
            value = value - jnp.where(me >= distance, incoming[slot, chunk, 0], 0.0)
            value = value - jnp.where(me < n - distance, incoming[slot, chunk, 1], 0.0)
        state[:, place] = value
        return value

    def place_of(chunk):
        return slice(chunk * width, (chunk + 1) * width)

    def first_level(solve):
        pair = split(state[...])
        for chunk in range(CHUNKS):
            for way in range(2):
                outgoing[0, chunk, way] = times(pair, factors[way, :, place_of(chunk)])
            send(solve, 0, chunk)

    def middle_level(solve, level):
        parity = level % 2
        totals = {}
        for part in range(CHUNKS):
            pair = split(received(solve, level - 1, part))
            for chunk in range(CHUNKS):
                for way in range(2):
                    term = times(pair, factors[way, place_of(part), place_of(chunk)])
                    key = (chunk, way)
                    totals[key] = totals[key] + term if part else term
                    if part == CHUNKS - 1:
                        outgoing[parity, chunk, way] = totals[key]
                if part == CHUNKS - 1:
                    send(solve, level, chunk)
        sent(level - 1)

    def last_level(solve):
        level = levels - 1
        parity = level % 2
        side = jnp.where(me >= n // 2, 1, 0)
        totals = {}
        for part in range(CHUNKS):
            pair = split(received(solve, level - 1, part))
            for chunk in range(CHUNKS):
                term = times(pair, factors[side, place_of(part), place_of(chunk)])
                totals[chunk] = totals[chunk] + term if part else term
                if part == CHUNKS - 1:
                    outgoing[parity, chunk, 0] = totals[chunk]
                    send(solve, level, chunk)
        sent(level - 1)

    def final_part(solve):
        total = None
        for part in range(CHUNKS):
            pair = split(received(solve, levels - 1, part))
            term = times(pair, diagonal[place_of(part), :])
            total = total + term if part else term
        sent(levels - 1)
        return total

    def near_start(step):
        local = lax.dot_general(
            basis[...],
            basis[...],
            (((1,), (1,)), ((), ())),
            precision=lax.Precision.HIGHEST,
            preferred_element_type=jnp.float32,
        ) * (1.0 / unknowns)
        for k in range(4):
            near_parts[step, spot, :, k * BASIS : (k + 1) * BASIS] = local[k * PANEL : (k + 1) * PANEL]
        mine = near_parts.at[step, spot]
        for target in near:
            pltpu.make_async_remote_copy(
                src_ref=mine,
                dst_ref=mine,
                send_sem=near_send.at[step],
                recv_sem=near_receive.at[step],
                device_id=(target,),
                device_id_type=MESH,
            ).start()

    def settle(parts, step, count, sem):
        some = parts.at[step, pl.ds(0, count)]
        pltpu.make_async_copy(some, some, sem.at[step]).wait()

    def far_start(step):
        settle(near_parts, step, group - 1, near_receive)
        far_parts[step, plane] = jnp.sum(near_parts[step], axis=0)
        mine = far_parts.at[step, plane]
        for target in far:
            pltpu.make_async_remote_copy(
                src_ref=mine,
                dst_ref=mine,
                send_sem=far_send.at[step],
                recv_sem=far_receive.at[step],
                device_id=(target,),
                device_id_type=MESH,
            ).start()
        settle(near_parts, step, group - 1, near_send)

    def expand(step):
        settle(far_parts, step, others - 1, far_receive)
        total = jnp.sum(far_parts[step], axis=0)
        for k in range(4):
            gram[k * PANEL : (k + 1) * PANEL, :] = total[:, k * BASIS : (k + 1) * BASIS]
        cross = gram[0:PANEL, :]
        rest = gram[PANEL:BASIS, :]
        through = jnp.zeros_like(cross)
        tall = jnp.zeros_like(rest)
        for k in range(PANEL, BASIS):
            through = through + cross[:, k : k + 1] * gram[k : k + 1, :]
            tall = tall + rest[:, k : k + 1] * gram[k : k + 1, :]
        both = 2.0 * cross - through
        tall = 2.0 * rest - tall
        again = jnp.zeros_like(cross)
        for k in range(PANEL, BASIS):
            again = again + both[:, k : k + 1] * gram[k : k + 1, :]
        left = cross - again
        square = cross - again
        for k in range(PANEL, BASIS):
            square = square - left[:, k : k + 1] * tall[k - PANEL : k - PANEL + 1, :]
        square = square + jnp.where(lane8 == row8, EPSILON, 0.0)
        mixed = jnp.where(lane8 < PANEL, jnp.where(lane8 == row8, 1.0, 0.0), -both)
        for k in range(PANEL):
            scale = lax.rsqrt(square[k : k + 1, k : k + 1])
            upper = square[k : k + 1, :] * scale
            mixed_row = mixed[k : k + 1, :] * scale
            column = square[:, k : k + 1] * scale
            square = jnp.where(row8 > k, square - column * upper, jnp.where(row8 == k, upper, square))
            mixed = jnp.where(row8 > k, mixed - column * mixed_row, jnp.where(row8 == k, mixed_row, mixed))
        upper = jnp.where(lane8 >= row8, square, 0.0)
        mixing[...] = mixed
        height = pl.multiple_of(PANEL * (step + 1), PANEL)
        zeros = jnp.zeros((PANEL, PANEL), jnp.float32)
        coefficients_ref[step, 0 : BASIS - PANEL, :] = tall[:, :PANEL]
        coefficients_ref[step, BASIS - PANEL : BASIS, :] = zeros
        coefficients_ref[step, pl.ds(height, PANEL), :] = upper[:, :PANEL]
        firsts_ref[step, 0 : BASIS - PANEL, :] = rest[:, :PANEL]
        firsts_ref[step, BASIS - PANEL : BASIS, :] = zeros
        fresh = combine(mixed, basis)
        panels_ref[pl.ds(pl.multiple_of(PANEL * step, PANEL), PANEL), :] = fresh
        settle(far_parts, step, others - 1, far_send)
        return fresh

    def after(solve, level):
        if level == hooks[0]:

            @pl.when(solve > 0)
            def _():
                near_start(solve - 1)

        if level == hooks[1]:

            @pl.when(solve > 0)
            def _():
                far_start(solve - 1)

        if level == hooks[2]:

            @pl.when(solve > 0)
            def _():
                fresh = expand(solve - 1)
                basis[pl.ds(pl.multiple_of(PANEL * (solve + 1), PANEL), PANEL), :] = fresh

    @pl.loop(0, STEPS)
    def _(solve):
        first_level(solve)
        after(solve, 0)
        for level in range(1, levels - 1):
            middle_level(solve, level)
            after(solve, level)
        last_level(solve)

        @pl.when(solve == 0)
        def _():
            loads[3].wait()

        images[0:PANEL, :] = final_part(solve)
        image = combine(mixing[...], images)
        state[...] = image
        basis[0:PANEL, :] = image
        images[pl.ds(pl.multiple_of(PANEL * (solve + 1), PANEL), PANEL), :] = image

    near_start(STEPS - 1)
    far_start(STEPS - 1)
    expand(STEPS - 1)


def arnoldi(n, group, hooks, start_panel, diagonal_inverse, right_factor, left_factor):
    columns = start_panel.shape[1]
    width = columns // CHUNKS
    levels = n.bit_length() - 1
    others = n // group
    vmem = pl.BlockSpec(memory_space=pltpu.VMEM)
    anywhere = pl.BlockSpec(memory_space=pl.ANY)
    dma = pltpu.SemaphoreType.DMA
    return pl.pallas_call(
        functools.partial(kernel, n, group, hooks),
        out_shape=(
            jax.ShapeDtypeStruct((STEPS * PANEL, columns), jnp.float32),
            jax.ShapeDtypeStruct((STEPS, BASIS, PANEL), jnp.float32),
            jax.ShapeDtypeStruct((STEPS, BASIS, PANEL), jnp.float32),
        ),
        in_specs=[anywhere] * 4,
        out_specs=(vmem, vmem, vmem),
        scratch_shapes=[
            pltpu.VMEM((2, columns, columns), jnp.bfloat16),
            pltpu.VMEM((columns, columns), jnp.bfloat16),
            pltpu.VMEM((PANEL, columns), jnp.float32),
            pltpu.VMEM((2, CHUNKS, 2, PANEL, width), jnp.float32),
            pltpu.VMEM((STEPS * levels, CHUNKS, 2, PANEL, width), jnp.float32),
            pltpu.VMEM((BASIS, columns), jnp.float32),
            pltpu.VMEM((BASIS, columns), jnp.float32),
            pltpu.VMEM((PANEL, BASIS), jnp.float32),
            pltpu.VMEM((BASIS, BASIS), jnp.float32),
            pltpu.VMEM((STEPS, group, PANEL, 4 * BASIS), jnp.float32),
            pltpu.VMEM((STEPS, others, PANEL, 4 * BASIS), jnp.float32),
            dma((4,)),
            dma((2,)),
            dma((STEPS * levels, CHUNKS)),
            dma((STEPS,)),
            dma((STEPS,)),
            dma((STEPS,)),
            dma((STEPS,)),
        ],
        compiler_params=pltpu.CompilerParams(
            collective_id=0, has_side_effects=True, vmem_limit_bytes=40 * 1024 * 1024
        ),
    )(start_panel, diagonal_inverse, right_factor, left_factor)


def solution(mesh):
    n = mesh.shape["rows"]
    group = 2 ** ((n.bit_length() - 1) // 2)
    hooks = (0, 2, 3) if n >= 64 else (0, 1, 2)
    placed = (P(None, "rows"), P("rows", None, None), P("rows", None, None), P("rows", None, None))
    return jax.shard_map(
        functools.partial(arnoldi, n, group, hooks),
        mesh=mesh,
        in_specs=placed,
        out_specs=(P(None, "rows"), P(), P()),
        check_vma=False,
    )
```

time: 406 us -> 149 us (0.37)
  starting transfers between devices: 167 us -> 0 us
  Pallas kernels: 0 us -> 141 us
  waiting for transfers between devices: 117 us -> 0 us
  blocking collectives: 70.2 us -> 0 us
  matrix products: 30.6 us -> 0 us
  other arithmetic: 10.2 us -> 0 us
    ppermute x48 -> x0, starting transfers between devices: 144 us -> none  [passed_along(): lax.ppermute(value, axis, [(source, source + steps) for source in range(i...]
    pallas_call x0 -> x1, Pallas kernels: none -> 141 us  [arnoldi(): pl.pallas_call(functools.partial(kernel, n, group, hooks), out_shape=(jax...]
    ppermute x48 -> x0, waiting for transfers between devices: 103 us -> none  [passed_along(): lax.ppermute(value, axis, [(source, source + steps) for source in range(i...]
    all_to_all x4 -> x0, blocking collectives: 70.2 us -> none  [from_everyone(): lax.all_to_all(jnp.broadcast_to(shard[None], (size, *shard.shape)), axis,...]
    dot_general x78 -> x0, matrix products: 29.9 us -> none  [the longest x24 9.95 us: cyclic_solve(): jnp.dot(lowered, right_factor[0], preferred_element_type=jnp.float32)]
    all_to_all x2 -> x0, starting transfers between devices: 22.1 us -> none  [from_everyone(): lax.all_to_all(jnp.broadcast_to(shard[None], (size, *shard.shape)), axis,...]
    all_to_all x2 -> x0, waiting for transfers between devices: 13.7 us -> none  [from_everyone(): lax.all_to_all(jnp.broadcast_to(shard[None], (size, *shard.shape)), axis,...]
    another operation x16 -> x0, other arithmetic: 8.66 us -> none  [the longest x9 4.23 us: body(): lower_factor = jnp.linalg.cholesky(gram_new)]
  transfers between devices with their start and end apart: 50 -> 0, of which waited for: 26 -> 0; matrix products, arithmetic and copies ran while one was open for 0% -> 0% of each run, Pallas kernels for 0% -> 0%
where the time goes in v1:
time: 149 us
  Pallas kernels  141 us (95%)
  local copies, waits for them, and re-layouts  7.51 us (5%)
    pallas_call x1, Pallas kernels, arnoldi(): pl.pallas_call(functools.partial(kernel, n, group, hooks), out_shape=(jax...  141 us
    unnamed x9, local copies, waits for them, and re-layouts  6.16 us

profile of v1, /device:TPU:1, one launch (start us, length us, event | category | flops | bytes accessed | tf_op | source)
XLA Modules:
  0.0 149.1 jit_solution(15712636348748390304)
XLA Ops:
  0.6 0.0 copy-start
  0.6 1.6 %copy-done = bf16[1,1024,1024]{2,1,0:T(8,128)(2,1)S(1)} copy-done((bf16[1,1024,1024]{2,1,0:T(8,128)(2,1)S(1)}, bf16[1,1024,1024]{2,1,0:T(8,128)(2,1)}, u32[]{:S(2)}) %copy-start) | copy-done | bytes 2097176
  2.2 0.0 copy-start.1
  2.2 1.6 %copy-done.1 = bf16[1,1024,1024]{2,1,0:T(8,128)(2,1)S(1)} copy-done((bf16[1,1024,1024]{2,1,0:T(8,128)(2,1)S(1)}, bf16[1,1024,1024]{2,1,0:T(8,128)(2,1)}, u32[]{:S(2)}) %copy-start.1) | copy-done | bytes 2097176
  3.8 0.0 copy-start.2
  3.8 1.6 %copy-done.2 = bf16[1,1024,1024]{2,1,0:T(8,128)(2,1)S(1)} copy-done((bf16[1,1024,1024]{2,1,0:T(8,128)(2,1)S(1)}, bf16[1,1024,1024]{2,1,0:T(8,128)(2,1)}, u32[]{:S(2)}) %copy-start.2) | copy-done | bytes 2097176
  5.4 0.0 copy-start.3
  5.4 0.8 copy-done.3
  6.2 140.9 %shard_map.67 = (f32[24,1024]{1,0:T(8,128)S(1)}, f32[3,32,8]{2,1,0:T(8,128)S(1)}, f32[3,32,8]{2,1,0:T(8,128)S(1)}) custom-call(f32[8,1024]{1,0:T(8,128)S(1)} %copy-done.3, bf16[1,1024,1024]{2,1,0:T(8,128)(2,1)S(1)} %copy-done, bf16[1,1024,1024]{2,1,0:T(8,128)(2,1)S(1)} %copy-done.1, bf16[1,1024,1024]{2,1,0:T(8,128)(2,1)S(1)} %copy-done.2), custom_call_target="tpu_custom_call" | custom-call | tf_op jit(solution)/shard_map/pallas_call | solution.py:333
  147.1 0.7 copy.7
  147.8 0.7 copy.8
  148.5 0.6 copy.10
Async XLA Ops:
  0.6 1.6 %copy-start = (bf16[1,1024,1024]{2,1,0:T(8,128)(2,1)S(1)}, bf16[1,1024,1024]{2,1,0:T(8,128)(2,1)}, u32[]{:S(2)}) copy-start(bf16[1,1024,1024]{2,1,0:T(8,128)(2,1)} %diagonal_hbm.1) | copy-start | bytes 6291460
  2.2 1.6 %copy-start.1 = (bf16[1,1024,1024]{2,1,0:T(8,128)(2,1)S(1)}, bf16[1,1024,1024]{2,1,0:T(8,128)(2,1)}, u32[]{:S(2)}) copy-start(bf16[1,1024,1024]{2,1,0:T(8,128)(2,1)} %right_hbm.1) | copy-start | bytes 6291460
  3.8 1.6 %copy-start.2 = (bf16[1,1024,1024]{2,1,0:T(8,128)(2,1)S(1)}, bf16[1,1024,1024]{2,1,0:T(8,128)(2,1)}, u32[]{:S(2)}) copy-start(bf16[1,1024,1024]{2,1,0:T(8,128)(2,1)} %left_hbm.1) | copy-start | bytes 6291460
  5.4 0.8 copy-start.3

commit v2 on v1

--- a/solution.py
+++ b/solution.py
@@ -10,8 +10,10 @@
 STEPS = 3
 BASIS = 32
 PANEL = 8
-CHUNKS = 4
+CUTS = (0, 512, 1024)
+SPLITS = (CUTS,) * 8
 EPSILON = 1e-06
+VMEM_GRANT = 54 * 1024 * 1024
 MESH = pl.DeviceIdType.MESH
 
 
@@ -64,7 +66,6 @@
 ):
     me = lax.axis_index("rows")
     columns = state.shape[1]
-    width = columns // CHUNKS
     levels = n.bit_length() - 1
     unknowns = n * columns
     others = n // group
@@ -87,13 +88,11 @@
     barrier = pltpu.get_barrier_semaphore()
     near = [lane_start + lax.rem(spot + k, group) for k in range(1, group)]
     far = [spot + group * lax.rem(plane + k, others) for k in range(1, others)]
-    across = []
-    distance = 1
-    while distance < group:
-        across += [peer(distance), peer(-distance)]
-        distance *= 2
-    for target in near + far + across:
-        pl.semaphore_signal(barrier, inc=1, device_id=(target,), device_id_type=MESH)
+    for way, offset, sends, _ in ((0, 1, me < n - 1, None), (1, -1, me >= 1, None)):
+
+        @pl.when(sends)
+        def _():
+            pl.semaphore_signal(barrier, inc=1, device_id=(peer(offset),), device_id_type=MESH)
 
     row8 = lax.broadcasted_iota(jnp.int32, (PANEL, BASIS), 0)
     lane8 = lax.broadcasted_iota(jnp.int32, (PANEL, BASIS), 1)
@@ -102,94 +101,100 @@
     mixing[...] = jnp.where(lane8 == row8, 1.0, 0.0)
     loads[2].wait()
     basis[PANEL : 2 * PANEL, :] = state[...]
-    pl.semaphore_wait(barrier, len(near) + len(far) + len(across))
     loads[0].wait()
     loads[1].wait()
 
+    def place_of(level, chunk):
+        return slice(*SPLITS[level][chunk : chunk + 2])
+
+    def ways_of(level):
+        distance = 2**level
+        if level == levels - 1:
+            return ((0, distance, None, None),)
+        return (
+            (0, distance, me < n - distance, me >= distance),
+            (1, -distance, me >= distance, me < n - distance),
+        )
+
+    def where_needed(condition, action):
+        if condition is None:
+            action()
+        else:
+            pl.when(condition)(action)
+
     def send(solve, level, chunk):
         slot = solve * levels + level
-        parity = level % 2
-        distance = 2**level
-        last = level == levels - 1
-        for way, offset in ((0, distance),) if last else ((0, distance), (1, -distance)):
-            pltpu.make_async_remote_copy(
-                src_ref=outgoing.at[parity, chunk, way],
-                dst_ref=incoming.at[slot, chunk, way],
-                send_sem=send_sems.at[parity],
-                recv_sem=receive_sems.at[slot, chunk],
+        place = place_of(level, chunk)
+        for way, offset, sends, _ in ways_of(level):
+            copy = pltpu.make_async_remote_copy(
+                src_ref=outgoing.at[level % 2, way, :, place],
+                dst_ref=incoming.at[slot, way, :, place],
+                send_sem=send_sems.at[level % 2, way],
+                recv_sem=receive_sems.at[slot, chunk, way],
                 device_id=(peer(offset),),
                 device_id_type=MESH,
-            ).start()
+            )
+            where_needed(sends, copy.start)
 
     def sent(level):
-        parity = level % 2
-        whole = outgoing.at[parity, :, 0] if level == levels - 1 else outgoing.at[parity]
-        pltpu.make_async_copy(whole, whole, send_sems.at[parity]).wait()
+        for way, _, sends, _ in ways_of(level):
+            whole = outgoing.at[level % 2, way]
+            where_needed(sends, pltpu.make_async_copy(whole, whole, send_sems.at[level % 2, way]).wait)
 
     def received(solve, level, chunk):
         slot = solve * levels + level
-        distance = 2**level
-        place = slice(chunk * width, (chunk + 1) * width)
-        if level == levels - 1:
-            arrived = incoming.at[slot, chunk, 0]
-        else:
-            arrived = incoming.at[slot, chunk]
-        pltpu.make_async_copy(arrived, arrived, receive_sems.at[slot, chunk]).wait()
+        place = place_of(level, chunk)
         value = state[:, place]
-        if level == levels - 1:
-            value = value - incoming[slot, chunk, 0]
-        else:
-            value = value - jnp.where(me >= distance, incoming[slot, chunk, 0], 0.0)
-            value = value - jnp.where(me < n - distance, incoming[slot, chunk, 1], 0.0)
+        for way, _, _, takes in ways_of(level):
+            arrived = incoming.at[slot, way, :, place]
+            where_needed(takes, pltpu.make_async_copy(arrived, arrived, receive_sems.at[slot, chunk, way]).wait)
+        for way, _, _, takes in ways_of(level):
+            update = incoming[slot, way, :, place]
+            value = value - (update if takes is None else jnp.where(takes, update, 0.0))
         state[:, place] = value
         return value
 
-    def place_of(chunk):
-        return slice(chunk * width, (chunk + 1) * width)
-
-    def first_level(solve):
+    def first_level(solve, entering):
         pair = split(state[...])
-        for chunk in range(CHUNKS):
+        for chunk in range(len(SPLITS[0]) - 1):
             for way in range(2):
-                outgoing[0, chunk, way] = times(pair, factors[way, :, place_of(chunk)])
+                place = place_of(0, chunk)
+                outgoing[0, way, :, place] = times(pair, factors[way, :, place])
+            if entering:
+                continue
             send(solve, 0, chunk)
-
-    def middle_level(solve, level):
+        if entering:
+            pl.semaphore_wait(barrier, jnp.where(me >= 1, 1, 0) + jnp.where(me < n - 1, 1, 0))
+            for chunk in range(len(SPLITS[0]) - 1):
+                send(solve, 0, chunk)
+
+    def next_level(solve, level):
         parity = level % 2
+        if level == levels - 1:
+            sides = ((0, jnp.where(me >= n // 2, 1, 0)),)
+        else:
+            sides = ((0, 0), (1, 1))
         totals = {}
-        for part in range(CHUNKS):
+        parts = len(SPLITS[level - 1]) - 1
+        for part in range(parts):
             pair = split(received(solve, level - 1, part))
-            for chunk in range(CHUNKS):
-                for way in range(2):
-                    term = times(pair, factors[way, place_of(part), place_of(chunk)])
-                    key = (chunk, way)
-                    totals[key] = totals[key] + term if part else term
-                    if part == CHUNKS - 1:
-                        outgoing[parity, chunk, way] = totals[key]
-                if part == CHUNKS - 1:
+            rows = place_of(level - 1, part)
+            for chunk in range(len(SPLITS[level]) - 1):
+                place = place_of(level, chunk)
+                for way, side in sides:
+                    term = times(pair, factors[side, rows, place])
+                    totals[chunk, way] = totals[chunk, way] + term if part else term
+                    if part == parts - 1:
+                        outgoing[parity, way, :, place] = totals[chunk, way]
+                if part == parts - 1:
                     send(solve, level, chunk)
         sent(level - 1)
 
-    def last_level(solve):
-        level = levels - 1
-        parity = level % 2
-        side = jnp.where(me >= n // 2, 1, 0)
-        totals = {}
-        for part in range(CHUNKS):
-            pair = split(received(solve, level - 1, part))
-            for chunk in range(CHUNKS):
-                term = times(pair, factors[side, place_of(part), place_of(chunk)])
-                totals[chunk] = totals[chunk] + term if part else term
-                if part == CHUNKS - 1:
-                    outgoing[parity, chunk, 0] = totals[chunk]
-                    send(solve, level, chunk)
-        sent(level - 1)
-
     def final_part(solve):
         total = None
-        for part in range(CHUNKS):
+        for part in range(len(SPLITS[levels - 1]) - 1):
             pair = split(received(solve, levels - 1, part))
-            term = times(pair, diagonal[place_of(part), :])
+            term = times(pair, diagonal[place_of(levels - 1, part), :])
             total = total + term if part else term
         sent(levels - 1)
         return total
@@ -257,22 +262,20 @@
             square = square - left[:, k : k + 1] * tall[k - PANEL : k - PANEL + 1, :]
         square = square + jnp.where(lane8 == row8, EPSILON, 0.0)
         mixed = jnp.where(lane8 < PANEL, jnp.where(lane8 == row8, 1.0, 0.0), -both)
+        lower = jnp.zeros_like(cross)
         for k in range(PANEL):
             scale = lax.rsqrt(square[k : k + 1, k : k + 1])
             upper = square[k : k + 1, :] * scale
             mixed_row = mixed[k : k + 1, :] * scale
             column = square[:, k : k + 1] * scale
+            lower = jnp.where(lane8 % PANEL == k, jnp.where(row8 >= k, column, 0.0), lower)
             square = jnp.where(row8 > k, square - column * upper, jnp.where(row8 == k, upper, square))
             mixed = jnp.where(row8 > k, mixed - column * mixed_row, jnp.where(row8 == k, mixed_row, mixed))
-        upper = jnp.where(lane8 >= row8, square, 0.0)
         mixing[...] = mixed
-        height = pl.multiple_of(PANEL * (step + 1), PANEL)
         zeros = jnp.zeros((PANEL, PANEL), jnp.float32)
-        coefficients_ref[step, 0 : BASIS - PANEL, :] = tall[:, :PANEL]
-        coefficients_ref[step, BASIS - PANEL : BASIS, :] = zeros
-        coefficients_ref[step, pl.ds(height, PANEL), :] = upper[:, :PANEL]
-        firsts_ref[step, 0 : BASIS - PANEL, :] = rest[:, :PANEL]
-        firsts_ref[step, BASIS - PANEL : BASIS, :] = zeros
+        here = lane8 // PANEL == step + 1
+        coefficients_ref[step] = jnp.concatenate([both[:, PANEL:], zeros], 1) + jnp.where(here, lower, 0.0)
+        firsts_ref[step] = jnp.concatenate([cross[:, PANEL:], zeros], 1)
         fresh = combine(mixed, basis)
         panels_ref[pl.ds(pl.multiple_of(PANEL * step, PANEL), PANEL), :] = fresh
         settle(far_parts, step, others - 1, far_send)
@@ -298,14 +301,18 @@
                 fresh = expand(solve - 1)
                 basis[pl.ds(pl.multiple_of(PANEL * (solve + 1), PANEL), PANEL), :] = fresh
 
+    first_level(0, True)
+
     @pl.loop(0, STEPS)
     def _(solve):
-        first_level(solve)
+        @pl.when(solve > 0)
+        def _():
+            first_level(solve, False)
+
         after(solve, 0)
-        for level in range(1, levels - 1):
-            middle_level(solve, level)
+        for level in range(1, levels):
+            next_level(solve, level)
             after(solve, level)
-        last_level(solve)
 
         @pl.when(solve == 0)
         def _():
@@ -322,29 +329,35 @@
     expand(STEPS - 1)
 
 
+def publish(panels_ref, coefficients_ref, firsts_ref, panels_out, coefficients_out, firsts_out):
+    pairs = ((panels_ref, panels_out), (coefficients_ref, coefficients_out), (firsts_ref, firsts_out))
+    for source, target in pairs:
+        target[...] = source[...]
+
+
 def arnoldi(n, group, hooks, start_panel, diagonal_inverse, right_factor, left_factor):
     columns = start_panel.shape[1]
-    width = columns // CHUNKS
     levels = n.bit_length() - 1
     others = n // group
     vmem = pl.BlockSpec(memory_space=pltpu.VMEM)
     anywhere = pl.BlockSpec(memory_space=pl.ANY)
     dma = pltpu.SemaphoreType.DMA
-    return pl.pallas_call(
+    shapes = (
+        jax.ShapeDtypeStruct((STEPS * PANEL, columns), jnp.float32),
+        jax.ShapeDtypeStruct((STEPS, PANEL, BASIS), jnp.float32),
+        jax.ShapeDtypeStruct((STEPS, PANEL, BASIS), jnp.float32),
+    )
+    results = pl.pallas_call(
         functools.partial(kernel, n, group, hooks),
-        out_shape=(
-            jax.ShapeDtypeStruct((STEPS * PANEL, columns), jnp.float32),
-            jax.ShapeDtypeStruct((STEPS, BASIS, PANEL), jnp.float32),
-            jax.ShapeDtypeStruct((STEPS, BASIS, PANEL), jnp.float32),
-        ),
+        out_shape=shapes,
         in_specs=[anywhere] * 4,
         out_specs=(vmem, vmem, vmem),
         scratch_shapes=[
             pltpu.VMEM((2, columns, columns), jnp.bfloat16),
             pltpu.VMEM((columns, columns), jnp.bfloat16),
             pltpu.VMEM((PANEL, columns), jnp.float32),
-            pltpu.VMEM((2, CHUNKS, 2, PANEL, width), jnp.float32),
-            pltpu.VMEM((STEPS * levels, CHUNKS, 2, PANEL, width), jnp.float32),
+            pltpu.VMEM((2, 2, PANEL, columns), jnp.float32),
+            pltpu.VMEM((STEPS * levels, 2, PANEL, columns), jnp.float32),
             pltpu.VMEM((BASIS, columns), jnp.float32),
             pltpu.VMEM((BASIS, columns), jnp.float32),
             pltpu.VMEM((PANEL, BASIS), jnp.float32),
@@ -352,17 +365,25 @@
             pltpu.VMEM((STEPS, group, PANEL, 4 * BASIS), jnp.float32),
             pltpu.VMEM((STEPS, others, PANEL, 4 * BASIS), jnp.float32),
             dma((4,)),
-            dma((2,)),
-            dma((STEPS * levels, CHUNKS)),
+            dma((2, 2)),
+            dma((STEPS * levels, max(len(cuts) for cuts in SPLITS), 2)),
             dma((STEPS,)),
             dma((STEPS,)),
             dma((STEPS,)),
             dma((STEPS,)),
         ],
         compiler_params=pltpu.CompilerParams(
-            collective_id=0, has_side_effects=True, vmem_limit_bytes=40 * 1024 * 1024
+            collective_id=0, has_side_effects=True, vmem_limit_bytes=VMEM_GRANT
         ),
     )(start_panel, diagonal_inverse, right_factor, left_factor)
+    panels, coefficients, firsts = pl.pallas_call(
+        publish,
+        out_shape=shapes,
+        in_specs=[vmem] * 3,
+        out_specs=(vmem,) * 3,
+        name="publish",
+    )(*results)
+    return panels, jnp.swapaxes(coefficients, 1, 2), jnp.swapaxes(firsts, 1, 2)
 
 
 def solution(mesh):

time: 149 us -> 133 us (0.89)
  Pallas kernels: 141 us -> 132 us
  local copies, waits for them, and re-layouts: 7.51 us -> 0 us
    pallas_call x1 -> x2, Pallas kernels: 141 us -> 132 us  [the longest x1 131 us: arnoldi(): pl.pallas_call(functools.partial(kernel, n, group, hooks), out_shape=shap...]
    unnamed x9 -> x0, local copies, waits for them, and re-layouts: 6.16 us -> none
where the time goes in v2:
time: 133 us
  Pallas kernels  132 us (99%)
    pallas_call x1, Pallas kernels, arnoldi(): pl.pallas_call(functools.partial(kernel, n, group, hooks), out_shape=shap...  131 us

profile of v2, /device:TPU:1, one launch (start us, length us, event | category | flops | bytes accessed | tf_op | source)
XLA Modules:
  0.0 133.1 jit_solution(6353297708250273425)
XLA Ops:
  0.6 130.9 %shard_map.67 = (f32[24,1024]{1,0:T(8,128)}, f32[3,8,32]{2,1,0:T(8,128)}, f32[3,8,32]{2,1,0:T(8,128)}) custom-call(f32[8,1024]{1,0:T(8,128)} %start_hbm.1, bf16[1,1024,1024]{2,1,0:T(8,128)(2,1)} %diagonal_hbm.1, bf16[1,1024,1024]{2,1,0:T(8,128)(2,1)} %right_hbm.1, bf16[1,1024,1024]{2,1,0:T(8,128)(2,1)} %left_hbm.1), custom_call_target="tpu_custom_call" | custom-call | tf_op jit(solution)/shard_map/pallas_call | solution.py:350
  131.5 1.6 %publish.1 = (f32[24,1024]{1,0:T(8,128)}, f32[3,8,32]{2,1,0:T(8,128)}, f32[3,8,32]{2,1,0:T(8,128)}) custom-call(f32[24,1024]{1,0:T(8,128)} %get-tuple-element.9.panels_ref, f32[3,8,32]{2,1,0:T(8,128)} %get-tuple-element.10.coefficients_ref, f32[3,8,32]{2,1,0:T(8,128)} %get-tuple-element.11.firsts_ref), custom_call_target="tpu_custom_call" | custom-call | tf_op jit(solution)/shard_map/publish/pallas_call | solution.py:379

commit v3 on v2

--- a/solution.py
+++ b/solution.py
@@ -10,10 +10,11 @@
 STEPS = 3
 BASIS = 32
 PANEL = 8
-CUTS = (0, 512, 1024)
-SPLITS = (CUTS,) * 8
+HALVES = (0, 512, 1024)
+QUARTERS = (0, 256, 512, 768, 1024)
+SPLITS = (HALVES,) * 8
 EPSILON = 1e-06
-VMEM_GRANT = 54 * 1024 * 1024
+VMEM_GRANT = 53 * 1024 * 1024
 MESH = pl.DeviceIdType.MESH
 
 
@@ -27,9 +28,9 @@
     return both[:PANEL] + both[PANEL:]
 
 
-def combine(weights, rows_ref):
-    total = weights[:, 0:1] * rows_ref[0:1, :]
-    for b in range(1, BASIS):
+def combine(weights, rows_ref, start=0, stop=BASIS):
+    total = weights[:, start : start + 1] * rows_ref[start : start + 1, :]
+    for b in range(start + 1, stop):
         total = total + weights[:, b : b + 1] * rows_ref[b : b + 1, :]
     return total
 
@@ -52,6 +53,7 @@
     incoming,
     basis,
     images,
+    known,
     mixing,
     gram,
     near_parts,
@@ -76,18 +78,23 @@
     def peer(offset):
         return lax.rem(me + (offset + n), n)
 
-    loads = [
-        pltpu.make_async_copy(right_hbm.at[0], factors.at[0], load_sems.at[0]),
-        pltpu.make_async_copy(left_hbm.at[0], factors.at[1], load_sems.at[1]),
-        pltpu.make_async_copy(start_hbm, state, load_sems.at[2]),
-        pltpu.make_async_copy(diagonal_hbm.at[0], diagonal, load_sems.at[3]),
-    ]
-    for load in (loads[2], loads[0], loads[1], loads[3]):
-        load.start()
+    load_start = pltpu.make_async_copy(start_hbm, state, load_sems.at[8])
+    load_diagonal = pltpu.make_async_copy(diagonal_hbm.at[0], diagonal, load_sems.at[9])
+    loads = []
+    load_start.start()
+    for chunk in range(len(SPLITS[0]) - 1):
+        for way, factor in ((0, right_hbm), (1, left_hbm)):
+            place = slice(*SPLITS[0][chunk : chunk + 2])
+            load = pltpu.make_async_copy(factor.at[0, :, place], factors.at[way, :, place], load_sems.at[len(loads)])
+            load.start()
+            loads.append(load)
+    load_diagonal.start()
 
     barrier = pltpu.get_barrier_semaphore()
-    near = [lane_start + lax.rem(spot + k, group) for k in range(1, group)]
-    far = [spot + group * lax.rem(plane + k, others) for k in range(1, others)]
+    in_line = sorted(range(1, group), key=lambda k: -min(k, group - k))
+    in_plane = sorted(range(1, others), key=lambda k: -min(k % 4, 4 - k % 4) - min(k // 4, 4 - k // 4))
+    near = [spot + group * lax.rem(plane + k, others) for k in in_plane]
+    far = [lane_start + lax.rem(spot + k, group) for k in in_line]
     for way, offset, sends, _ in ((0, 1, me < n - 1, None), (1, -1, me >= 1, None)):
 
         @pl.when(sends)
@@ -98,11 +105,10 @@
     lane8 = lax.broadcasted_iota(jnp.int32, (PANEL, BASIS), 1)
     basis[...] = jnp.zeros_like(basis)
     images[...] = jnp.zeros_like(images)
+    known[...] = jnp.zeros_like(known)
     mixing[...] = jnp.where(lane8 == row8, 1.0, 0.0)
-    loads[2].wait()
+    load_start.wait()
     basis[PANEL : 2 * PANEL, :] = state[...]
-    loads[0].wait()
-    loads[1].wait()
 
     def place_of(level, chunk):
         return slice(*SPLITS[level][chunk : chunk + 2])
@@ -116,25 +122,33 @@
             (1, -distance, me >= distance, me < n - distance),
         )
 
+    def urgent(level):
+        distance = 2**level
+        stretch = group if distance < group else group * 4
+        return jnp.where(lax.rem(me, stretch) < distance, 1, 0)
+
     def where_needed(condition, action):
         if condition is None:
             action()
         else:
             pl.when(condition)(action)
 
-    def send(solve, level, chunk):
+    def send(solve, level, chunk, way):
         slot = solve * levels + level
         place = place_of(level, chunk)
-        for way, offset, sends, _ in ways_of(level):
-            copy = pltpu.make_async_remote_copy(
-                src_ref=outgoing.at[level % 2, way, :, place],
-                dst_ref=incoming.at[slot, way, :, place],
-                send_sem=send_sems.at[level % 2, way],
-                recv_sem=receive_sems.at[slot, chunk, way],
-                device_id=(peer(offset),),
-                device_id_type=MESH,
-            )
-            where_needed(sends, copy.start)
+        offset = 2**level if level == levels - 1 else 2**level * (1 - 2 * way)
+        copy = pltpu.make_async_remote_copy(
+            src_ref=outgoing.at[level % 2, way, :, place],
+            dst_ref=incoming.at[slot, way, :, place],
+            send_sem=send_sems.at[level % 2, way],
+            recv_sem=receive_sems.at[slot, chunk, way],
+            device_id=(peer(offset),),
+            device_id_type=MESH,
+        )
+        if level == levels - 1:
+            copy.start()
+        else:
+            pl.when(jnp.logical_and(me + offset >= 0, me + offset < n))(copy.start)
 
     def sent(level):
         for way, _, sends, _ in ways_of(level):
@@ -156,38 +170,40 @@
 
     def first_level(solve, entering):
         pair = split(state[...])
-        for chunk in range(len(SPLITS[0]) - 1):
-            for way in range(2):
-                place = place_of(0, chunk)
-                outgoing[0, way, :, place] = times(pair, factors[way, :, place])
+        first = 0 if entering else urgent(0)
+        pieces = [(way, chunk) for chunk in range(len(SPLITS[0]) - 1) for way in (first, 1 - first)]
+        for number, (way, chunk) in enumerate(pieces):
+            place = place_of(0, chunk)
             if entering:
-                continue
-            send(solve, 0, chunk)
+                loads[number].wait()
+            outgoing[0, way, :, place] = times(pair, factors[way, :, place])
+            if not entering:
+                send(solve, 0, chunk, way)
         if entering:
             pl.semaphore_wait(barrier, jnp.where(me >= 1, 1, 0) + jnp.where(me < n - 1, 1, 0))
-            for chunk in range(len(SPLITS[0]) - 1):
-                send(solve, 0, chunk)
+            for way, chunk in pieces:
+                send(solve, 0, chunk, way)
 
     def next_level(solve, level):
         parity = level % 2
+        first = urgent(level)
         if level == levels - 1:
             sides = ((0, jnp.where(me >= n // 2, 1, 0)),)
         else:
-            sides = ((0, 0), (1, 1))
+            sides = ((first, first), (1 - first, 1 - first))
         totals = {}
         parts = len(SPLITS[level - 1]) - 1
         for part in range(parts):
             pair = split(received(solve, level - 1, part))
             rows = place_of(level - 1, part)
             for chunk in range(len(SPLITS[level]) - 1):
-                place = place_of(level, chunk)
-                for way, side in sides:
+                for number, (way, side) in enumerate(sides):
+                    place = place_of(level, chunk)
                     term = times(pair, factors[side, rows, place])
-                    totals[chunk, way] = totals[chunk, way] + term if part else term
+                    totals[number, chunk] = totals[number, chunk] + term if part else term
                     if part == parts - 1:
-                        outgoing[parity, way, :, place] = totals[chunk, way]
-                if part == parts - 1:
-                    send(solve, level, chunk)
+                        outgoing[parity, way, :, place] = totals[number, chunk]
+                        send(solve, level, chunk, way)
         sent(level - 1)
 
     def final_part(solve):
@@ -208,8 +224,8 @@
             preferred_element_type=jnp.float32,
         ) * (1.0 / unknowns)
         for k in range(4):
-            near_parts[step, spot, :, k * BASIS : (k + 1) * BASIS] = local[k * PANEL : (k + 1) * PANEL]
-        mine = near_parts.at[step, spot]
+            near_parts[step, plane, :, k * BASIS : (k + 1) * BASIS] = local[k * PANEL : (k + 1) * PANEL]
+        mine = near_parts.at[step, plane]
         for target in near:
             pltpu.make_async_remote_copy(
                 src_ref=mine,
@@ -225,9 +241,9 @@
         pltpu.make_async_copy(some, some, sem.at[step]).wait()
 
     def far_start(step):
-        settle(near_parts, step, group - 1, near_receive)
-        far_parts[step, plane] = jnp.sum(near_parts[step], axis=0)
-        mine = far_parts.at[step, plane]
+        settle(near_parts, step, others - 1, near_receive)
+        far_parts[step, spot] = jnp.sum(near_parts[step], axis=0)
+        mine = far_parts.at[step, spot]
         for target in far:
             pltpu.make_async_remote_copy(
                 src_ref=mine,
@@ -237,10 +253,10 @@
                 device_id=(target,),
                 device_id_type=MESH,
             ).start()
-        settle(near_parts, step, group - 1, near_send)
+        settle(near_parts, step, others - 1, near_send)
 
     def expand(step):
-        settle(far_parts, step, others - 1, far_receive)
+        settle(far_parts, step, group - 1, far_receive)
         total = jnp.sum(far_parts[step], axis=0)
         for k in range(4):
             gram[k * PANEL : (k + 1) * PANEL, :] = total[:, k * BASIS : (k + 1) * BASIS]
@@ -278,7 +294,7 @@
         firsts_ref[step] = jnp.concatenate([cross[:, PANEL:], zeros], 1)
         fresh = combine(mixed, basis)
         panels_ref[pl.ds(pl.multiple_of(PANEL * step, PANEL), PANEL), :] = fresh
-        settle(far_parts, step, others - 1, far_send)
+        settle(far_parts, step, group - 1, far_send)
         return fresh
 
     def after(solve, level):
@@ -300,6 +316,7 @@
             def _():
                 fresh = expand(solve - 1)
                 basis[pl.ds(pl.multiple_of(PANEL * (solve + 1), PANEL), PANEL), :] = fresh
+                known[...] = combine(mixing[...], images, PANEL)
 
     first_level(0, True)
 
@@ -316,10 +333,10 @@
 
         @pl.when(solve == 0)
         def _():
-            loads[3].wait()
+            load_diagonal.wait()
 
         images[0:PANEL, :] = final_part(solve)
-        image = combine(mixing[...], images)
+        image = combine(mixing[...], images, 0, PANEL) + known[...]
         state[...] = image
         basis[0:PANEL, :] = image
         images[pl.ds(pl.multiple_of(PANEL * (solve + 1), PANEL), PANEL), :] = image
@@ -360,11 +377,12 @@
             pltpu.VMEM((STEPS * levels, 2, PANEL, columns), jnp.float32),
             pltpu.VMEM((BASIS, columns), jnp.float32),
             pltpu.VMEM((BASIS, columns), jnp.float32),
+            pltpu.VMEM((PANEL, columns), jnp.float32),
             pltpu.VMEM((PANEL, BASIS), jnp.float32),
             pltpu.VMEM((BASIS, BASIS), jnp.float32),
+            pltpu.VMEM((STEPS, others, PANEL, 4 * BASIS), jnp.float32),
             pltpu.VMEM((STEPS, group, PANEL, 4 * BASIS), jnp.float32),
-            pltpu.VMEM((STEPS, others, PANEL, 4 * BASIS), jnp.float32),
-            dma((4,)),
+            dma((10,)),
             dma((2, 2)),
             dma((STEPS * levels, max(len(cuts) for cuts in SPLITS), 2)),
             dma((STEPS,)),
@@ -382,6 +400,7 @@
         in_specs=[vmem] * 3,
         out_specs=(vmem,) * 3,
         name="publish",
+        compiler_params=pltpu.CompilerParams(vmem_limit_bytes=1024 * 1024),
     )(*results)
     return panels, jnp.swapaxes(coefficients, 1, 2), jnp.swapaxes(firsts, 1, 2)
 
@@ -389,7 +408,7 @@
 def solution(mesh):
     n = mesh.shape["rows"]
     group = 2 ** ((n.bit_length() - 1) // 2)
-    hooks = (0, 2, 3) if n >= 64 else (0, 1, 2)
+    hooks = (0, 4, 6) if n >= 64 else (0, 1, 2)
     placed = (P(None, "rows"), P("rows", None, None), P("rows", None, None), P("rows", None, None))
     return jax.shard_map(
         functools.partial(arnoldi, n, group, hooks),

time: 133 us -> 132 us (level)
  Pallas kernels: 132 us -> 130 us
    pallas_call x1, Pallas kernels: 131 us -> 130 us  [arnoldi(): pl.pallas_call(functools.partial(kernel, n, group, hooks), out_shape=shap...]
where the time goes in v3:
time: 132 us
  Pallas kernels  130 us (98%)
    pallas_call x1, Pallas kernels, arnoldi(): pl.pallas_call(functools.partial(kernel, n, group, hooks), out_shape=shap...  130 us

profile of v3, /device:TPU:1, one launch (start us, length us, event | category | flops | bytes accessed | tf_op | source)
XLA Modules:
  0.0 131.6 jit_solution(16958928001295667347)
XLA Ops:
  0.6 0.0 copy-start
  0.6 0.7 copy-done
  1.4 129.5 %shard_map.67 = (f32[24,1024]{1,0:T(8,128)S(1)}, f32[3,8,32]{2,1,0:T(8,128)S(1)}, f32[3,8,32]{2,1,0:T(8,128)S(1)}) custom-call(f32[8,1024]{1,0:T(8,128)S(1)} %copy-done, bf16[1,1024,1024]{2,1,0:T(8,128)(2,1)} %diagonal_hbm.1, bf16[1,1024,1024]{2,1,0:T(8,128)(2,1)} %right_hbm.1, bf16[1,1024,1024]{2,1,0:T(8,128)(2,1)} %left_hbm.1), custom_call_target="tpu_custom_call" | custom-call | tf_op jit(solution)/shard_map/pallas_call | solution.py:367
  130.9 0.7 publish.1
Async XLA Ops:
  0.6 0.8 copy-start

commit v4 on v3

--- a/solution.py
+++ b/solution.py
@@ -408,7 +408,7 @@
 def solution(mesh):
     n = mesh.shape["rows"]
     group = 2 ** ((n.bit_length() - 1) // 2)
-    hooks = (0, 4, 6) if n >= 64 else (0, 1, 2)
+    hooks = (1, 4, 6) if n >= 64 else (0, 1, 2)
     placed = (P(None, "rows"), P("rows", None, None), P("rows", None, None), P("rows", None, None))
     return jax.shard_map(
         functools.partial(arnoldi, n, group, hooks),

time: 132 us -> 131 us (level)
  no operation moved by 1% of the time
where the time goes in v4:
time: 131 us
  Pallas kernels  129 us (98%)
    pallas_call x1, Pallas kernels, arnoldi(): pl.pallas_call(functools.partial(kernel, n, group, hooks), out_shape=shap...  129 us

profile of v4, /device:TPU:1, one launch (start us, length us, event | category | flops | bytes accessed | tf_op | source)
XLA Modules:
  0.0 130.8 jit_solution(3990319551141011217)
XLA Ops:
  0.6 0.0 copy-start
  0.6 0.7 copy-done
  1.4 128.7 %shard_map.67 = (f32[24,1024]{1,0:T(8,128)S(1)}, f32[3,8,32]{2,1,0:T(8,128)S(1)}, f32[3,8,32]{2,1,0:T(8,128)S(1)}) custom-call(f32[8,1024]{1,0:T(8,128)S(1)} %copy-done, bf16[1,1024,1024]{2,1,0:T(8,128)(2,1)} %diagonal_hbm.1, bf16[1,1024,1024]{2,1,0:T(8,128)(2,1)} %right_hbm.1, bf16[1,1024,1024]{2,1,0:T(8,128)(2,1)} %left_hbm.1), custom_call_target="tpu_custom_call" | custom-call | tf_op jit(solution)/shard_map/pallas_call | solution.py:367
  130.1 0.7 publish.1
Async XLA Ops:
  0.6 0.8 copy-start

commit v5 on v4

--- a/solution.py
+++ b/solution.py
@@ -28,11 +28,15 @@
     return both[:PANEL] + both[PANEL:]
 
 
+def in_quarters(terms):
+    sums = list(terms[:4])
+    for i, term in enumerate(terms[4:]):
+        sums[i % 4] = sums[i % 4] + term
+    return (sums[0] + sums[1]) + (sums[2] + sums[3])
+
+
 def combine(weights, rows_ref, start=0, stop=BASIS):
-    total = weights[:, start : start + 1] * rows_ref[start : start + 1, :]
-    for b in range(start + 1, stop):
-        total = total + weights[:, b : b + 1] * rows_ref[b : b + 1, :]
-    return total
+    return in_quarters([weights[:, b : b + 1] * rows_ref[b : b + 1, :] for b in range(start, stop)])
 
 
 def kernel(
@@ -262,20 +266,12 @@
             gram[k * PANEL : (k + 1) * PANEL, :] = total[:, k * BASIS : (k + 1) * BASIS]
         cross = gram[0:PANEL, :]
         rest = gram[PANEL:BASIS, :]
-        through = jnp.zeros_like(cross)
-        tall = jnp.zeros_like(rest)
-        for k in range(PANEL, BASIS):
-            through = through + cross[:, k : k + 1] * gram[k : k + 1, :]
-            tall = tall + rest[:, k : k + 1] * gram[k : k + 1, :]
+        span = range(PANEL, BASIS)
+        through = in_quarters([cross[:, k : k + 1] * gram[k : k + 1, :] for k in span])
+        tall = 2.0 * rest - in_quarters([rest[:, k : k + 1] * gram[k : k + 1, :] for k in span])
         both = 2.0 * cross - through
-        tall = 2.0 * rest - tall
-        again = jnp.zeros_like(cross)
-        for k in range(PANEL, BASIS):
-            again = again + both[:, k : k + 1] * gram[k : k + 1, :]
-        left = cross - again
-        square = cross - again
-        for k in range(PANEL, BASIS):
-            square = square - left[:, k : k + 1] * tall[k - PANEL : k - PANEL + 1, :]
+        left = cross - in_quarters([both[:, k : k + 1] * gram[k : k + 1, :] for k in span])
+        square = left - in_quarters([left[:, k : k + 1] * tall[k - PANEL : k - PANEL + 1, :] for k in span])
         square = square + jnp.where(lane8 == row8, EPSILON, 0.0)
         mixed = jnp.where(lane8 < PANEL, jnp.where(lane8 == row8, 1.0, 0.0), -both)
         lower = jnp.zeros_like(cross)

time: 131 us -> 131 us (level)
  no operation moved by 1% of the time
where the time goes in v5:
time: 131 us
  Pallas kernels  129 us (98%)
    pallas_call x1, Pallas kernels, arnoldi(): pl.pallas_call(functools.partial(kernel, n, group, hooks), out_shape=shap...  129 us

profile of v5, /device:TPU:1, one launch (start us, length us, event | category | flops | bytes accessed | tf_op | source)
XLA Modules:
  0.0 130.8 jit_solution(7529382871525185071)
XLA Ops:
  0.6 0.0 copy-start
  0.6 0.7 copy-done
  1.4 128.7 %shard_map.67 = (f32[24,1024]{1,0:T(8,128)S(1)}, f32[3,8,32]{2,1,0:T(8,128)S(1)}, f32[3,8,32]{2,1,0:T(8,128)S(1)}) custom-call(f32[8,1024]{1,0:T(8,128)S(1)} %copy-done, bf16[1,1024,1024]{2,1,0:T(8,128)(2,1)} %diagonal_hbm.1, bf16[1,1024,1024]{2,1,0:T(8,128)(2,1)} %right_hbm.1, bf16[1,1024,1024]{2,1,0:T(8,128)(2,1)} %left_hbm.1), custom_call_target="tpu_custom_call" | custom-call | tf_op jit(solution)/shard_map/pallas_call | solution.py:363
  130.1 0.7 publish.1
Async XLA Ops:
  0.6 0.8 copy-start
